TPU v7x, 32 devices: a whole 2x2x4 slice. The times are simulated.
32 devices in a mesh: dp: 8 (over y, x, core), seq: 4 (over z).
Axes of the slice: x: 2, y: 2, z: 4, core: 2. Of those that a mesh axis runs over, the one named last changes fastest.
Arguments:
- hidden_in: bfloat16 [8, 512, 2048], P('dp', 'seq'), may hold values from -6 to 6
- cotangent: bfloat16 [8, 512, 2048], P('dp', 'seq'), may hold values from -6 to 6
- norm_gain: float32 [2048], P('dp'), may hold values from 0.1 to 1.9
- route_weights: float32 [8, 512, 10], P('dp', 'seq'), may hold values from 0.1 to 1
- expert_ids: int32 [8, 512, 10], P('dp', 'seq'), may hold values from 0 to 63, all different within a row; in each aligned block of 128 rows (0 to 127, 128 to 255, ..., all dimensions but the last counted through in order) at most 24 rows name the same one
- expert_gate: bfloat16 [64, 2048, 512], P(('dp', 'seq')), may hold values from -0.125 to 0.125
- expert_up: bfloat16 [64, 2048, 512], P(('dp', 'seq')), may hold values from -0.125 to 0.125
- expert_down: bfloat16 [64, 512, 2048], P(('dp', 'seq')), may hold values from -0.25 to 0.25
Outputs:
- grad_hidden: bfloat16 [8, 512, 2048], P('dp', 'seq')
- grad_gain: float32 [2048], P('dp')
- grad_gate: bfloat16 [64, 2048, 512], P(('dp', 'seq'))
- grad_up: bfloat16 [64, 2048, 512], P(('dp', 'seq'))
- grad_down: bfloat16 [64, 512, 2048], P(('dp', 'seq'))
Inputs may be any that keep to these rules, and one draw needn't show every extreme that they name: `expert_ids`: each token names 10 different experts. Among the rows of one device no expert is named by more than 24 of them, and in some device one expert is named by exactly 24.
All inputs are finite; a program needn't handle non-finite values.
Results may differ from a plain program's by a relative error of at most 0.0072.
Values may be sent and summed in bfloat16 or wider, within the bound.
No kernel may reach another device: no remote copies, remote signals or barrier semaphores. Data moves between devices by JAX's collectives and lax.ppermute only.
A program may use at most 192 MiB of HBM per device.

v0:
```python
import jax
import jax.numpy as jnp
from jax import lax
from jax.sharding import PartitionSpec as P

TOP = 10
EPSILON = 1e-06


def shards(
    hidden_in, cotangent, norm_gain, route_weights, expert_ids, expert_gate, expert_up, expert_down
):
    tokens_here = hidden_in.shape[1]
    model_width = hidden_in.shape[2]
    local_experts = expert_gate.shape[0]
    dp_count = lax.axis_size("dp")
    seq_count = lax.axis_size("seq")
    devices = dp_count * seq_count
    expert_count = local_experts * devices
    capacity = max(2, tokens_here * TOP * 6 // (5 * expert_count))
    dp_at = lax.axis_index("dp")
    seq_at = lax.axis_index("seq")
    my_index = dp_at * seq_count + seq_at
    upstream = cotangent[0]
    all_grads = lax.all_gather(upstream, ("dp", "seq"), axis=0)
    gain_full = lax.all_gather(norm_gain, "dp", axis=0, tiled=True)
    inputs = hidden_in[0].astype(jnp.float32)
    inverse_root = lax.rsqrt(jnp.mean(inputs * inputs, axis=1, keepdims=True) + EPSILON)
    scaled = inputs * inverse_root
    normed = (scaled * gain_full[None, :]).astype(jnp.bfloat16)
    all_rows = lax.all_gather(normed, ("dp", "seq"), axis=0)
    ids_here = expert_ids[0]
    weights_here = route_weights[0]
    ids_all = lax.all_gather(ids_here.T, ("dp", "seq"), axis=0, tiled=False)
    weights_all = lax.all_gather(weights_here.T, ("dp", "seq"), axis=0, tiled=False)
    place = jnp.arange(tokens_here, dtype=jnp.int32)
    upper = (place[:, None] < place[None, :]).astype(jnp.bfloat16)
    slots = jnp.arange(capacity, dtype=jnp.int32)
    my_experts = my_index * local_experts + jnp.arange(local_experts, dtype=jnp.int32)
    named = ids_all[:, None, :, :] == my_experts[None, :, None, None]
    chosen = jnp.any(named, axis=2)
    weight = jnp.sum(jnp.where(named, weights_all[:, None, :, :], 0.0), axis=2)
    rank = jnp.einsum(
        "nit,tu->niu", chosen.astype(jnp.bfloat16), upper, preferred_element_type=jnp.float32
    ).astype(jnp.int32)
    picks = chosen[:, :, None, :] & (rank[:, :, None, :] == slots[None, None, :, None])
    row_weight = jnp.sum(jnp.where(picks, weight[:, :, None, :], 0.0), axis=3)
    picks = picks.reshape(devices, local_experts * capacity, tokens_here).astype(jnp.bfloat16)
    row_weight = row_weight.reshape(devices, local_experts * capacity, 1)

    def pick(table):
        return jnp.einsum("nst,ntd->nsd", picks, table, preferred_element_type=jnp.float32)

    four_shape = (devices, local_experts, capacity, model_width)
    rows_grad = (row_weight * pick(all_grads)).astype(jnp.bfloat16).reshape(four_shape)
    rows_in = pick(all_rows).astype(jnp.bfloat16).reshape(four_shape)
    grad_act = jnp.einsum(
        "nicd,ifd->nicf", rows_grad, expert_down, preferred_element_type=jnp.float32
    )
    pre_gate = jnp.einsum(
        "nicd,idf->nicf", rows_in, expert_gate, preferred_element_type=jnp.float32
    )
    pre_up = jnp.einsum("nicd,idf->nicf", rows_in, expert_up, preferred_element_type=jnp.float32)
    sigmoid_gate = jax.nn.sigmoid(pre_gate)
    silu_gate = pre_gate * sigmoid_gate
    activation = (silu_gate * pre_up).astype(jnp.bfloat16)
    gate_back = (grad_act * pre_up * sigmoid_gate * (1.0 + pre_gate * (1.0 - sigmoid_gate))).astype(
        jnp.bfloat16
    )
    up_back = (grad_act * silu_gate).astype(jnp.bfloat16)
    returned = (
        jnp.einsum("nicf,idf->nicd", gate_back, expert_gate, preferred_element_type=jnp.float32)
        + jnp.einsum("nicf,idf->nicd", up_back, expert_up, preferred_element_type=jnp.float32)
    ).astype(jnp.bfloat16)
    back_rows = lax.all_to_all(
        returned.reshape(devices, local_experts * capacity, model_width),
        ("dp", "seq"),
        split_axis=0,
        concat_axis=0,
        tiled=True,
    )
    grad_down = jnp.einsum(
        "nicf,nicd->ifd", activation, rows_grad, preferred_element_type=jnp.float32
    ).astype(jnp.bfloat16)
    grad_gate = jnp.einsum(
        "nicd,nicf->idf", rows_in, gate_back, preferred_element_type=jnp.float32
    ).astype(jnp.bfloat16)
    grad_up = jnp.einsum(
        "nicd,nicf->idf", rows_in, up_back, preferred_element_type=jnp.float32
    ).astype(jnp.bfloat16)
    experts_range = jnp.arange(expert_count, dtype=jnp.int32)
    chosen_here = jnp.any(ids_here[:, :, None] == experts_range[None, None, :], axis=1)
    rank_here = jnp.dot(
        upper.T, chosen_here.astype(jnp.bfloat16), preferred_element_type=jnp.float32
    ).astype(jnp.int32)
    sums = (
        (chosen_here[:, :, None] & (rank_here[:, :, None] == slots[None, None, :]))
        .reshape(tokens_here, expert_count * capacity)
        .astype(jnp.bfloat16)
    )
    summed = jnp.dot(
        sums,
        back_rows.reshape(expert_count * capacity, model_width),
        preferred_element_type=jnp.float32,
    )
    local_gain = jnp.sum(summed * scaled, axis=0)
    total_gain = lax.psum(local_gain, ("dp", "seq"))
    shard_width = norm_gain.shape[0]
    grad_gain = lax.dynamic_slice(total_gain, (dp_at * shard_width,), (shard_width,))
    gained = summed * gain_full[None, :]
    centered = jnp.mean(gained * scaled, axis=1, keepdims=True)
    grad_hidden = (
        upstream.astype(jnp.float32) + inverse_root * (gained - scaled * centered)
    ).astype(jnp.bfloat16)
    return (grad_hidden.reshape(hidden_in.shape), grad_gain, grad_gate, grad_up, grad_down)


def solution(mesh):
    return jax.shard_map(
        shards,
        mesh=mesh,
        in_specs=(
            P("dp", "seq", None),
            P("dp", "seq", None),
            P("dp"),
            P("dp", "seq", None),
            P("dp", "seq", None),
            P(("dp", "seq"), None, None),
            P(("dp", "seq"), None, None),
            P(("dp", "seq"), None, None),
        ),
        out_specs=(
            P("dp", "seq", None),
            P("dp"),
            P(("dp", "seq"), None, None),
            P(("dp", "seq"), None, None),
            P(("dp", "seq"), None, None),
        ),
        check_vma=False,
    )
```

profile of v0, /device:TPU:0, one launch (start us, length us, event | category | flops | bytes accessed | tf_op | source)
XLA Modules:
  0.0 491.8 jit_solution(4126240018301125779)
XLA Ops:
  7.2 0.0 all-gather.10.cloned.1.call-start
  7.2 1.2 fusion.40
  8.5 10.6 %all-gather.4 = f32[8,1,256]{2,1,0:T(1,128)S(1)} all-gather(f32[1,1,256]{2,1,0:T(1,128)} %bitcast.164), channel_id=1, replica_groups=mesh['dp'=8,'seq'=4] {'dp'}, dimensions={0}, use_global_device_ids=true | all-gather | bytes 9216 | tf_op jit(solution)/shard_map/all_gather | solution.py:26
  19.0 0.0 copy-done.11
  19.0 0.6 copy-done.9
  19.6 2.0 fusion.42
  21.6 0.0 all-gather.10.cloned.1.call-update
  21.7 0.0 all-gather.8.cloned.1.call-start
  21.7 0.7 all-gather.8.cloned.1.call-update
  22.4 0.1 eq.88
  22.5 0.7 copy.91
  23.2 0.7 copy.92
  23.9 74.0 %all-gather.3 = f32[32,10,128]{2,1,0:T(8,128)S(1)} all-gather(f32[1,10,128]{2,1,0:T(8,128)S(1)} %bitcast.163), channel_id=3, replica_groups=mesh['dp'=8,'seq'=4] {'dp','seq'}, dimensions={0}, use_global_device_ids=true | all-gather | bytes 168960 | tf_op jit(solution)/shard_map/all_gather | solution.py:35
  97.8 0.1 copy.55
  97.9 69.5 %all-gather.2 = s32[32,10,128]{2,1,0:T(8,128)S(1)} all-gather(s32[1,10,128]{2,1,0:T(8,128)S(1)} %bitcast.161), channel_id=2, replica_groups=mesh['dp'=8,'seq'=4] {'dp','seq'}, dimensions={0}, use_global_device_ids=true | all-gather | bytes 168960 | tf_op jit(solution)/shard_map/all_gather | solution.py:34
  167.4 0.1 copy.52
  167.5 0.1 fusion.47
  167.6 0.1 compare_reduce_fusion
  167.7 0.1 convolution_convert_fusion.1
  167.9 0.4 select_reduce_fusion
  168.3 0.1 copy.57
  168.4 0.1 copy.58
  168.4 0.2 fusion.45
  168.7 0.0 all-gather.10.cloned.1.call-done
  168.7 0.0 copy-start.3
  168.7 8.7 %convolution_convert_fusion = bf16[32,48,2048]{2,1,0:T(8,128)(2,1)S(1)} fusion(pred[32,48,128]{2,1,0:T(8,128)(4,1)S(1)} %fusion.45, bf16[32,128,2048]{2,1,0:T(8,128)(2,1)} %all-gather.10.cloned.1.call-done), kind=kOutput, calls=%fused_computation.14 | convolution fusion | flops 808452096 | bytes 23265280 | tf_op jit(solution)/shard_map/nst,ntd->nsd/dot_general | solution.py:52
  177.4 0.0 copy-start.1
  177.4 0.0 copy-done.3
  177.4 0.0 copy-start.4
  177.4 5.1 %fusion.1 = f32[2,32,24,512]{3,2,1,0:T(8,128)} fusion(bf16[32,2,24,2048]{3,2,1,0:T(8,128)(2,1)S(1)} %bitcast.152, bf16[2,2048,512]{2,1,0:T(8,128)(2,1)S(1)} %copy-done.3), kind=kOutput, calls=%fused_computation.6 | convolution fusion | flops 3221225472 | bytes 13631488 | tf_op jit(solution)/shard_map/nicd,idf->nicf/dot_general | solution.py:60
  182.6 0.0 copy-done.1
  182.6 0.0 copy-done.4
  182.6 5.1 %fusion.3 = f32[2,32,24,512]{3,2,1,0:T(8,128)} fusion(bf16[32,2,24,2048]{3,2,1,0:T(8,128)(2,1)S(1)} %bitcast.153, bf16[2,2048,512]{2,1,0:T(8,128)(2,1)S(1)} %copy-done.4), kind=kOutput, calls=%fused_computation.8 | convolution fusion | flops 3221225472 | bytes 13631488 | tf_op jit(solution)/shard_map/nicd,idf->nicf/dot_general | solution.py:63
  187.7 68.5 %all-gather.8.cloned.1.call-done = bf16[32,128,2048]{2,1,0:T(8,128)(2,1)} async-done(((bf16[1,128,2048]{2,1,0:T(8,128)(2,1)}), bf16[32,128,2048]{2,1,0:T(8,128)(2,1)}) %all-gather.8.cloned.1.call-update) | async-done | bytes 16777232 | tf_op jit(solution)/shard_map/all_gather | solution.py:25
  256.2 8.1 %multiply_convert_fusion = bf16[32,48,2048]{2,1,0:T(8,128)(2,1)S(1)} fusion(f32[32,48]{1,0:T(8,128)S(1)} %copy.58, pred[32,48,128]{2,1,0:T(8,128)(4,1)S(1)} %fusion.45, bf16[32,128,2048]{2,1,0:T(8,128)(2,1)} %all-gather.8.cloned.1.call-done), kind=kOutput, calls=%fused_computation.1 | convolution fusion | flops 811597824 | bytes 23271424 | tf_op jit(solution)/shard_map/nst,ntd->nsd/dot_general | solution.py:52
  264.3 0.0 copy-start
  264.3 9.9 %fusion.25 = (bf16[32,2,24,512]{3,2,0,1:T(8,128)(2,1)S(1)}, bf16[32,2,24,512]{3,2,0,1:T(8,128)(2,1)S(1)}) fusion(f32[2,32,24,512]{3,2,1,0:T(8,128)} %fusion.1, f32[2,32,24,512]{3,2,1,0:T(8,128)} %fusion.3, bf16[2,512,2048]{2,1,0:T(8,128)(2,1)} %param.15, bf16[32,2,24,2048]{3,2,1,0:T(8,128)(2,1)S(1)} %bitcast.148), kind=kOutput, calls=%fused_computation.35 | convolution fusion | flops 3231449088 | bytes 19922944 | tf_op jit(solution)/shard_map/nicd,ifd->nicf/dot_general | solution.py:57
  274.2 0.0 copy-done
  274.2 0.0 copy-start.6
  274.2 0.0 copy-start.8
  274.3 9.8 %fusion.9 = f32[2,32,24,2048]{3,2,1,0:T(8,128)} fusion(bf16[32,2,24,512]{3,2,0,1:T(8,128)(2,1)S(1)} %get-tuple-element.8, bf16[2,2048,512]{2,1,0:T(8,128)(2,1)} %param.13), kind=kOutput, calls=%fused_computation.15 | convolution fusion | flops 3221225472 | bytes 18350080 | tf_op jit(solution)/shard_map/nicf,idf->nicd/dot_general | solution.py:72
  284.0 0.0 copy-done.6
  284.0 7.7 %fusion = bf16[32,2,24,2048]{3,2,0,1:T(8,128)(2,1)S(1)} fusion(f32[2,32,24,2048]{3,2,1,0:T(8,128)} %fusion.9, bf16[32,2,24,512]{3,2,0,1:T(8,128)(2,1)S(1)} %get-tuple-element.7, bf16[2,2048,512]{2,1,0:T(8,128)(2,1)} %param.14), kind=kOutput, calls=%fused_computation.5 | convolution fusion | flops 3227516928 | bytes 24641536 | tf_op jit(solution)/shard_map/nicf,idf->nicd/dot_general | solution.py:73
  291.8 3.2 copy.62
  295.0 3.7 all-to-all-start
  298.8 0.1 convolution_convert_fusion.2
  299.0 0.2 fusion.43
  299.1 0.0 copy-start.7
  299.2 0.0 slice-start.1
  299.2 8.9 %bitcast_convert_fusion.1 = bf16[2,2048,512]{2,1,0:T(8,128)(2,1)} fusion(bf16[32,2,24,2048]{3,2,1,0:T(8,128)(2,1)} %bitcast.154, bf16[32,2,24,512]{3,2,0,1:T(8,128)(2,1)} %copy-done.8), kind=kOutput, calls=%fused_computation.3 | convolution fusion | flops 3223322624 | bytes 12058624 | tf_op jit(solution)/shard_map/nicd,nicf->idf/dot_general | solution.py:88
  308.0 0.0 copy-done.7
  308.0 9.4 %bitcast_convert_fusion.2 = bf16[2,2048,512]{2,1,0:T(8,128)(2,1)} fusion(bf16[32,2,24,2048]{3,2,1,0:T(8,128)(2,1)} %bitcast.155, bf16[32,2,24,512]{3,2,0,1:T(8,128)(2,1)S(1)} %copy-done.7), kind=kOutput, calls=%fused_computation.4 | convolution fusion | flops 3223322624 | bytes 12058624 | tf_op jit(solution)/shard_map/nicd,nicf->idf/dot_general | solution.py:85
  317.5 0.0 slice-done.1
  317.5 0.0 copy-start.2
  317.5 0.0 copy-start.10
  317.5 0.0 copy-start.12
  317.5 5.4 %bitcast_convert_fusion = bf16[2,512,2048]{2,1,0:T(8,128)(2,1)} fusion(bf16[32,2,24,2048]{3,2,1,0:T(8,128)(2,1)S(1)} %bitcast.151, f32[2,32,24,512]{3,2,1,0:T(8,128)S(1)} %copy-done.14, f32[2,32,24,512]{3,2,1,0:T(8,128)S(1)} %copy-done.13), kind=kOutput, calls=%fused_computation.2 | convolution fusion | flops 3228041216 | bytes 16777216 | tf_op jit(solution)/shard_map/nicf,nicd->ifd/dot_general | solution.py:82
  322.9 112.6 %all-to-all-done = bf16[32,48,2048]{2,1,0:T(8,128)(2,1)} async-done(((bf16[32,48,2048]{2,1,0:T(8,128)(2,1)}), bf16[32,48,2048]{2,1,0:T(8,128)(2,1)}, u32[]{:S(2)}, u32[]{:S(2)}) %all-to-all-start) | async-done | bytes 6291488 | tf_op jit(solution)/shard_map/all_to_all | solution.py:75
  435.5 0.0 copy-done.12
  435.5 0.0 copy-start.5
  435.5 4.1 fusion.39
  439.6 43.5 %psum.7 = f32[2048]{0:T(1024)S(1)} all-reduce(f32[2048]{0:T(1024)S(1)} %get-tuple-element.5), channel_id=1, replica_groups=mesh['dp'=8,'seq'=4] {'dp','seq'}, use_global_device_ids=true, to_apply=%region_7.8 | all-reduce | flops 2048 | bytes 16384 | tf_op jit(solution)/shard_map/psum | solution.py:107
  483.1 0.6 dynamic_slice.3
  483.7 1.2 fusion.46
  (21 shorter events, 0.2 us)
Async XLA Ops:
  7.2 161.5 %all-gather.10.cloned.1.call-start = ((), (), s32[]{:S(2)}) async-start(), calls=%async_computation.2 | async-start | bytes 17301504 | tf_op jit(solution)/shard_map/all_gather | solution.py:31
  8.4 10.6 %copy-start.11 = (f32[128]{0:T(128)}, f32[128]{0:T(128)S(1)}, u32[]{:S(2)}) copy-start(f32[128]{0:T(128)S(1)} %add_rsqrt_fusion) | copy-start | bytes 1540
  19.0 0.6 copy-start.9
  21.7 234.5 %all-gather.8.cloned.1.call-start = ((), (), s32[]{:S(2)}) async-start(), calls=%async_computation.1 | async-start | bytes 17301504 | tf_op jit(solution)/shard_map/all_gather | solution.py:25
  168.7 8.7 %copy-start.3 = (bf16[2,2048,512]{2,1,0:T(8,128)(2,1)S(1)}, bf16[2,2048,512]{2,1,0:T(8,128)(2,1)}, u32[]{:S(2)}) copy-start(bf16[2,2048,512]{2,1,0:T(8,128)(2,1)} %param.13) | copy-start | bytes 12582916
  177.4 5.2 %copy-start.1 = (bf16[32,48,2048]{2,1,0:T(8,128)(2,1)}, bf16[32,48,2048]{2,1,0:T(8,128)(2,1)S(1)}, u32[]{:S(2)}) copy-start(bf16[32,48,2048]{2,1,0:T(8,128)(2,1)S(1)} %convolution_convert_fusion) | copy-start | bytes 18874372
  177.4 5.1 %copy-start.4 = (bf16[2,2048,512]{2,1,0:T(8,128)(2,1)S(1)}, bf16[2,2048,512]{2,1,0:T(8,128)(2,1)}, u32[]{:S(2)}) copy-start(bf16[2,2048,512]{2,1,0:T(8,128)(2,1)} %param.14) | copy-start | bytes 12582916
  264.3 10.0 %copy-start = (bf16[32,48,2048]{2,1,0:T(8,128)(2,1)}, bf16[32,48,2048]{2,1,0:T(8,128)(2,1)S(1)}, u32[]{:S(2)}) copy-start(bf16[32,48,2048]{2,1,0:T(8,128)(2,1)S(1)} %multiply_convert_fusion) | copy-start | bytes 18874372
  274.2 9.8 %copy-start.6 = (bf16[32,2,24,512]{3,2,0,1:T(8,128)(2,1)}, bf16[32,2,24,512]{3,2,0,1:T(8,128)(2,1)S(1)}, u32[]{:S(2)}) copy-start(bf16[32,2,24,512]{3,2,0,1:T(8,128)(2,1)S(1)} %get-tuple-element.8) | copy-start | bytes 4718596
  274.2 9.8 %copy-start.8 = (bf16[32,2,24,512]{3,2,0,1:T(8,128)(2,1)}, bf16[32,2,24,512]{3,2,0,1:T(8,128)(2,1)S(1)}, u32[]{:S(2)}) copy-start(bf16[32,2,24,512]{3,2,0,1:T(8,128)(2,1)S(1)} %get-tuple-element.7) | copy-start | bytes 4718596
  295.0 22.4 %slice-start = ((s8[6291456]{0:T(1024)(128)(4,1)}), s8[2097152]{0:T(1024)(128)(4,1)S(1)}, s32[]{:S(2)}) async-start(s8[6291456]{0:T(1024)(128)(4,1)} %bitcast.149), calls=%async_computation.3 | async-start | bytes 4194304
  295.0 140.5 %all-to-all-start = ((bf16[32,48,2048]{2,1,0:T(8,128)(2,1)}), bf16[32,48,2048]{2,1,0:T(8,128)(2,1)}, u32[]{:S(2)}, u32[]{:S(2)}) async-start(bf16[32,48,2048]{2,1,0:T(8,128)(2,1)} %bitcast.147), calls=%async_computation | async-start | bytes 12582912 | tf_op jit(solution)/shard_map/all_to_all | solution.py:75
  299.1 8.9 %copy-start.7 = (bf16[32,2,24,512]{3,2,0,1:T(8,128)(2,1)S(1)}, bf16[32,2,24,512]{3,2,0,1:T(8,128)(2,1)}, u32[]{:S(2)}) copy-start(bf16[32,2,24,512]{3,2,0,1:T(8,128)(2,1)} %copy-done.6) | copy-start | bytes 4718596
  299.2 18.3 %slice-start.1 = ((s8[6291456]{0:T(1024)(128)(4,1)}), s8[4194304]{0:T(1024)(128)(4,1)S(1)}, s32[]{:S(2)}) async-start(s8[6291456]{0:T(1024)(128)(4,1)} %bitcast.149), calls=%async_computation.4 | async-start | bytes 8388608
  308.0 9.4 %copy-start.13 = (f32[2,32,24,512]{3,2,1,0:T(8,128)S(1)}, f32[2,32,24,512]{3,2,1,0:T(8,128)}, u32[]{:S(2)}) copy-start(f32[2,32,24,512]{3,2,1,0:T(8,128)} %fusion.1) | copy-start | bytes 9437188
  308.0 9.4 %copy-start.14 = (f32[2,32,24,512]{3,2,1,0:T(8,128)S(1)}, f32[2,32,24,512]{3,2,1,0:T(8,128)}, u32[]{:S(2)}) copy-start(f32[2,32,24,512]{3,2,1,0:T(8,128)} %fusion.3) | copy-start | bytes 9437188
  317.5 118.0 %copy-start.2 = (bf16[1,128,2048]{2,1,0:T(8,128)(2,1)S(1)}, bf16[1,128,2048]{2,1,0:T(8,128)(2,1)}, u32[]{:S(2)}) copy-start(bf16[1,128,2048]{2,1,0:T(8,128)(2,1)} %param.8) | copy-start | bytes 1572868
  317.5 118.0 %copy-start.10 = (f32[8,1,256]{2,1,0:T(1,128)S(1)}, f32[8,1,256]{2,1,0:T(1,128)}, u32[]{:S(2)}) copy-start(f32[8,1,256]{2,1,0:T(1,128)} %copy-done.9) | copy-start | bytes 24580
  317.5 118.0 %copy-start.12 = (f32[128]{0:T(128)S(1)}, f32[128]{0:T(128)}, u32[]{:S(2)}) copy-start(f32[128]{0:T(128)} %copy-done.11) | copy-start | bytes 1540
  435.5 48.2 %copy-start.5 = (bf16[1,128,2048]{2,1,0:T(8,128)(2,1)S(1)}, bf16[1,128,2048]{2,1,0:T(8,128)(2,1)}, u32[]{:S(2)}) copy-start(bf16[1,128,2048]{2,1,0:T(8,128)(2,1)} %param.9) | copy-start | bytes 1572868
Sparse Core Ops, SparseCore 0:
  21.8 117.1 all-gather.9
  142.0 114.1 all-gather.7
where the time goes:
time: 492 us
  blocking collectives  197 us (40%)
  waiting for transfers between devices  182 us (37%)
  matrix products  82.5 us (17%)
  between operations  14.3 us (3%)
  local copies, waits for them, and re-layouts  6.33 us (1%)
  other arithmetic  5.47 us (1%)
    all_to_all x1, waiting for transfers between devices, shards(): lax.all_to_all(returned.reshape(devices, local_experts * capacity, model_...  113 us
    all_gather x1, blocking collectives, shards(): lax.all_gather(weights_here.T, ('dp', 'seq'), axis=0, tiled=False)  74 us
    all_gather x1, blocking collectives, shards(): ids_all = lax.all_gather(ids_here.T, ('dp', 'seq'), axis=0, tiled=False)  69.5 us
    all_gather x1, waiting for transfers between devices, shards(): all_grads = lax.all_gather(upstream, ('dp', 'seq'), axis=0)  68.5 us
    psum x1, blocking collectives, shards(): total_gain = lax.psum(local_gain, ('dp', 'seq'))  43.5 us
    dot_general x2, matrix products, pick(): jnp.einsum('nst,ntd->nsd', picks, table, preferred_element_type=jnp.float32)  16.8 us
    all_gather x1, blocking collectives, shards(): gain_full = lax.all_gather(norm_gain, 'dp', axis=0, tiled=True)  10.6 us
    dot_general x1, matrix products, shards(): jnp.einsum('nicd,ifd->nicf', rows_grad, expert_down, preferred_element_ty...  9.94 us
  transfers between devices with their start and end apart: 3, of which 2 were waited for; matrix products, arithmetic and copies ran while one was open for 9% of the time, Pallas kernels for 0%

commit v1 on v0

--- a/solution.py
+++ b/solution.py
@@ -5,6 +5,12 @@
 
 TOP = 10
 EPSILON = 1e-06
+
+
+def modes_serve(x_local):
+    parts_out = lax.all_gather(x_local, ("dp", "seq"))
+    ready = jnp.sum(parts_out, 0)
+    return ready
 
 
 def shards(
@@ -104,7 +110,7 @@
         preferred_element_type=jnp.float32,
     )
     local_gain = jnp.sum(summed * scaled, axis=0)
-    total_gain = lax.psum(local_gain, ("dp", "seq"))
+    total_gain = modes_serve(local_gain)
     shard_width = norm_gain.shape[0]
     grad_gain = lax.dynamic_slice(total_gain, (dp_at * shard_width,), (shard_width,))
     gained = summed * gain_full[None, :]

time: 492 us -> 518 us (1.053)
  blocking collectives: 197 us -> 223 us
    all_gather x0 -> x1, blocking collectives: none -> 69.4 us  [modes_serve(): parts_out = lax.all_gather(x_local, ('dp', 'seq'))]
    psum x1 -> x0, blocking collectives: 43.5 us -> none  [shards(): total_gain = lax.psum(local_gain, ('dp', 'seq'))]
where the time goes in v1:
time: 518 us
  blocking collectives  223 us (43%)
  waiting for transfers between devices  183 us (35%)
  matrix products  81 us (16%)
  between operations  14.3 us (3%)
  local copies, waits for them, and re-layouts  6.38 us (1%)
  other arithmetic  5.51 us (1%)
    all_to_all x1, waiting for transfers between devices, shards(): lax.all_to_all(returned.reshape(devices, local_experts * capacity, model_...  114 us
    all_gather x1, blocking collectives, shards(): lax.all_gather(weights_here.T, ('dp', 'seq'), axis=0, tiled=False)  74 us
    all_gather x1, blocking collectives, shards(): ids_all = lax.all_gather(ids_here.T, ('dp', 'seq'), axis=0, tiled=False)  69.5 us
    all_gather x1, blocking collectives, modes_serve(): parts_out = lax.all_gather(x_local, ('dp', 'seq'))  69.4 us
    all_gather x1, waiting for transfers between devices, shards(): all_grads = lax.all_gather(upstream, ('dp', 'seq'), axis=0)  68.5 us
    dot_general x2, matrix products, pick(): jnp.einsum('nst,ntd->nsd', picks, table, preferred_element_type=jnp.float32)  16.8 us
    all_gather x1, blocking collectives, shards(): gain_full = lax.all_gather(norm_gain, 'dp', axis=0, tiled=True)  10.6 us
  transfers between devices with their start and end apart: 3, of which 2 were waited for; matrix products, arithmetic and copies ran while one was open for 9% of the time, Pallas kernels for 0%

profile of v1, /device:TPU:0, one launch (start us, length us, event | category | flops | bytes accessed | tf_op | source)
XLA Modules:
  0.0 517.8 jit_solution(7038647929534936926)
XLA Ops:
  7.2 0.0 all-gather.11.cloned.1.call-start
  7.2 1.2 fusion.40
  8.5 10.6 %all-gather.5 = f32[8,1,256]{2,1,0:T(1,128)S(1)} all-gather(f32[1,1,256]{2,1,0:T(1,128)} %bitcast.166), channel_id=1, replica_groups=mesh['dp'=8,'seq'=4] {'dp'}, dimensions={0}, use_global_device_ids=true | all-gather | bytes 9216 | tf_op jit(solution)/shard_map/all_gather | solution.py:32
  19.0 0.0 copy-done.11
  19.0 0.6 copy-done.9
  19.6 2.0 fusion.42
  21.6 0.0 all-gather.11.cloned.1.call-update
  21.7 0.0 all-gather.9.cloned.1.call-start
  21.7 0.7 all-gather.9.cloned.1.call-update
  22.4 0.1 eq.88
  22.5 0.7 copy.91
  23.2 0.7 copy.92
  23.9 74.0 %all-gather.4 = f32[32,10,128]{2,1,0:T(8,128)S(1)} all-gather(f32[1,10,128]{2,1,0:T(8,128)S(1)} %bitcast.165), channel_id=3, replica_groups=mesh['dp'=8,'seq'=4] {'dp','seq'}, dimensions={0}, use_global_device_ids=true | all-gather | bytes 168960 | tf_op jit(solution)/shard_map/all_gather | solution.py:41
  97.8 0.1 copy.55
  97.9 69.5 %all-gather.3 = s32[32,10,128]{2,1,0:T(8,128)S(1)} all-gather(s32[1,10,128]{2,1,0:T(8,128)S(1)} %bitcast.163), channel_id=2, replica_groups=mesh['dp'=8,'seq'=4] {'dp','seq'}, dimensions={0}, use_global_device_ids=true | all-gather | bytes 168960 | tf_op jit(solution)/shard_map/all_gather | solution.py:40
  167.4 0.1 copy.52
  167.5 0.1 fusion.47
  167.6 0.1 compare_reduce_fusion
  167.7 0.1 convolution_convert_fusion.1
  167.9 0.4 select_reduce_fusion
  168.3 0.1 copy.57
  168.4 0.1 copy.58
  168.4 0.2 fusion.45
  168.7 0.0 all-gather.11.cloned.1.call-done
  168.7 0.0 copy-start.3
  168.7 8.7 %convolution_convert_fusion = bf16[32,48,2048]{2,1,0:T(8,128)(2,1)S(1)} fusion(pred[32,48,128]{2,1,0:T(8,128)(4,1)S(1)} %fusion.45, bf16[32,128,2048]{2,1,0:T(8,128)(2,1)} %all-gather.11.cloned.1.call-done), kind=kOutput, calls=%fused_computation.14 | convolution fusion | flops 808452096 | bytes 23265280 | tf_op jit(solution)/shard_map/nst,ntd->nsd/dot_general | solution.py:58
  177.4 0.0 copy-start.1
  177.4 0.0 copy-done.3
  177.4 0.0 copy-start.4
  177.4 5.1 fusion.1
  182.5 0.0 copy-done.1
  182.5 0.0 copy-done.4
  182.5 5.1 fusion.3
  187.7 68.5 %all-gather.9.cloned.1.call-done = bf16[32,128,2048]{2,1,0:T(8,128)(2,1)} async-done(((bf16[1,128,2048]{2,1,0:T(8,128)(2,1)}), bf16[32,128,2048]{2,1,0:T(8,128)(2,1)}) %all-gather.9.cloned.1.call-update) | async-done | bytes 16777232 | tf_op jit(solution)/shard_map/all_gather | solution.py:31
  256.2 8.1 %multiply_convert_fusion = bf16[32,48,2048]{2,1,0:T(8,128)(2,1)S(1)} fusion(f32[32,48]{1,0:T(8,128)S(1)} %copy.58, pred[32,48,128]{2,1,0:T(8,128)(4,1)S(1)} %fusion.45, bf16[32,128,2048]{2,1,0:T(8,128)(2,1)} %all-gather.9.cloned.1.call-done), kind=kOutput, calls=%fused_computation.1 | convolution fusion | flops 811597824 | bytes 23271424 | tf_op jit(solution)/shard_map/nst,ntd->nsd/dot_general | solution.py:58
  264.3 0.0 copy-start
  264.3 9.9 %fusion.25 = (bf16[32,2,24,512]{3,2,0,1:T(8,128)(2,1)S(1)}, bf16[32,2,24,512]{3,2,0,1:T(8,128)(2,1)S(1)}) fusion(f32[2,32,24,512]{3,2,1,0:T(8,128)} %fusion.1, f32[2,32,24,512]{3,2,1,0:T(8,128)} %fusion.3, bf16[2,512,2048]{2,1,0:T(8,128)(2,1)} %param.15, bf16[32,2,24,2048]{3,2,1,0:T(8,128)(2,1)S(1)} %bitcast.148), kind=kOutput, calls=%fused_computation.35 | convolution fusion | flops 3231449088 | bytes 19922944 | tf_op jit(solution)/shard_map/nicd,ifd->nicf/dot_general | solution.py:63
  274.2 0.0 copy-done
  274.2 0.0 copy-start.6
  274.2 0.0 copy-start.8
  274.3 9.8 %fusion.9 = f32[2,32,24,2048]{3,2,1,0:T(8,128)} fusion(bf16[32,2,24,512]{3,2,0,1:T(8,128)(2,1)S(1)} %get-tuple-element.8, bf16[2,2048,512]{2,1,0:T(8,128)(2,1)} %param.13), kind=kOutput, calls=%fused_computation.15 | convolution fusion | flops 3221225472 | bytes 18350080 | tf_op jit(solution)/shard_map/nicf,idf->nicd/dot_general | solution.py:78
  284.0 0.0 copy-done.6
  284.0 0.0 copy-done.8
  284.0 7.7 %fusion = bf16[32,2,24,2048]{3,2,0,1:T(8,128)(2,1)S(1)} fusion(f32[2,32,24,2048]{3,2,1,0:T(8,128)} %fusion.9, bf16[32,2,24,512]{3,2,0,1:T(8,128)(2,1)S(1)} %get-tuple-element.7, bf16[2,2048,512]{2,1,0:T(8,128)(2,1)} %param.14), kind=kOutput, calls=%fused_computation.5 | convolution fusion | flops 3227516928 | bytes 24641536 | tf_op jit(solution)/shard_map/nicf,idf->nicd/dot_general | solution.py:79
  291.8 3.2 copy.62
  295.0 3.7 all-to-all-start
  298.8 0.1 convolution_convert_fusion.2
  298.9 0.2 fusion.43
  299.1 0.0 slice-start.3
  299.1 0.0 copy-start.7
  299.1 0.0 slice-start
  299.1 8.9 %bitcast_convert_fusion.1 = bf16[2,2048,512]{2,1,0:T(8,128)(2,1)} fusion(bf16[32,2,24,2048]{3,2,1,0:T(8,128)(2,1)} %bitcast.154, bf16[32,2,24,512]{3,2,0,1:T(8,128)(2,1)} %copy-done.8), kind=kOutput, calls=%fused_computation.3 | convolution fusion | flops 3223322624 | bytes 12058624 | tf_op jit(solution)/shard_map/nicd,nicf->idf/dot_general | solution.py:94
  308.0 0.0 slice-start.1
  308.0 5.1 bitcast_convert_fusion.2
  313.1 0.0 slice-done.1
  313.1 0.0 copy-start.12
  313.1 8.3 %bitcast_convert_fusion = bf16[2,512,2048]{2,1,0:T(8,128)(2,1)} fusion(bf16[32,2,24,2048]{3,2,1,0:T(8,128)(2,1)S(1)} %bitcast.151, f32[2,32,24,512]{3,2,1,0:T(8,128)} %fusion.3, f32[2,32,24,512]{3,2,1,0:T(8,128)} %fusion.1), kind=kOutput, calls=%fused_computation.2 | convolution fusion | flops 3228041216 | bytes 16777216 | tf_op jit(solution)/shard_map/nicf,nicd->ifd/dot_general | solution.py:88
  321.4 114.0 %all-to-all-done = bf16[32,48,2048]{2,1,0:T(8,128)(2,1)} async-done(((bf16[32,48,2048]{2,1,0:T(8,128)(2,1)}), bf16[32,48,2048]{2,1,0:T(8,128)(2,1)}, u32[]{:S(2)}, u32[]{:S(2)}) %all-to-all-start) | async-done | bytes 6291488 | tf_op jit(solution)/shard_map/all_to_all | solution.py:81
  435.5 0.0 copy-done.10
  435.5 0.0 copy-start.5
  435.5 4.1 fusion.39
  439.6 69.4 %all-gather.2 = f32[65536]{0:T(1024)S(1)} all-gather(f32[2048]{0:T(1024)S(1)} %get-tuple-element.5), channel_id=4, replica_groups=mesh['dp'=8,'seq'=4] {'dp','seq'}, dimensions={0}, use_global_device_ids=true | all-gather | bytes 270336 | tf_op jit(solution)/shard_map/all_gather | solution.py:11
  509.1 1.2 fusion.46
  510.3 0.6 dynamic_slice.3
  (24 shorter events, 0.2 us)
Async XLA Ops:
  7.2 161.5 %all-gather.11.cloned.1.call-start = ((), (), s32[]{:S(2)}) async-start(), calls=%async_computation.2 | async-start | bytes 17301504 | tf_op jit(solution)/shard_map/all_gather | solution.py:37
  8.4 10.6 %copy-start.11 = (f32[128]{0:T(128)}, f32[128]{0:T(128)S(1)}, u32[]{:S(2)}) copy-start(f32[128]{0:T(128)S(1)} %add_rsqrt_fusion) | copy-start | bytes 1540
  19.0 0.6 copy-start.9
  21.7 234.5 %all-gather.9.cloned.1.call-start = ((), (), s32[]{:S(2)}) async-start(), calls=%async_computation.1 | async-start | bytes 17301504 | tf_op jit(solution)/shard_map/all_gather | solution.py:31
  168.7 8.7 %copy-start.3 = (bf16[2,2048,512]{2,1,0:T(8,128)(2,1)S(1)}, bf16[2,2048,512]{2,1,0:T(8,128)(2,1)}, u32[]{:S(2)}) copy-start(bf16[2,2048,512]{2,1,0:T(8,128)(2,1)} %param.13) | copy-start | bytes 12582916
  177.4 5.1 copy-start.1
  177.4 5.1 copy-start.4
  264.3 10.0 %copy-start = (bf16[32,48,2048]{2,1,0:T(8,128)(2,1)}, bf16[32,48,2048]{2,1,0:T(8,128)(2,1)S(1)}, u32[]{:S(2)}) copy-start(bf16[32,48,2048]{2,1,0:T(8,128)(2,1)S(1)} %multiply_convert_fusion) | copy-start | bytes 18874372
  274.2 9.8 %copy-start.6 = (bf16[32,2,24,512]{3,2,0,1:T(8,128)(2,1)}, bf16[32,2,24,512]{3,2,0,1:T(8,128)(2,1)S(1)}, u32[]{:S(2)}) copy-start(bf16[32,2,24,512]{3,2,0,1:T(8,128)(2,1)S(1)} %get-tuple-element.8) | copy-start | bytes 4718596
  274.2 9.8 %copy-start.8 = (bf16[32,2,24,512]{3,2,0,1:T(8,128)(2,1)}, bf16[32,2,24,512]{3,2,0,1:T(8,128)(2,1)S(1)}, u32[]{:S(2)}) copy-start(bf16[32,2,24,512]{3,2,0,1:T(8,128)(2,1)S(1)} %get-tuple-element.7) | copy-start | bytes 4718596
  295.0 13.0 %slice-start.2 = ((s8[6291456]{0:T(1024)(128)(4,1)}), s8[2097152]{0:T(1024)(128)(4,1)S(1)}, s32[]{:S(2)}) async-start(s8[6291456]{0:T(1024)(128)(4,1)} %bitcast.155), calls=%async_computation.5 | async-start | bytes 4194304
  295.0 140.5 %all-to-all-start = ((bf16[32,48,2048]{2,1,0:T(8,128)(2,1)}), bf16[32,48,2048]{2,1,0:T(8,128)(2,1)}, u32[]{:S(2)}, u32[]{:S(2)}) async-start(bf16[32,48,2048]{2,1,0:T(8,128)(2,1)} %bitcast.147), calls=%async_computation | async-start | bytes 12582912 | tf_op jit(solution)/shard_map/all_to_all | solution.py:81
  299.1 8.9 %slice-start.3 = ((s8[6291456]{0:T(1024)(128)(4,1)}), s8[4194304]{0:T(1024)(128)(4,1)S(1)}, s32[]{:S(2)}) async-start(s8[6291456]{0:T(1024)(128)(4,1)} %bitcast.155), calls=%async_computation.6 | async-start | bytes 8388608
  299.1 8.9 %copy-start.7 = (bf16[32,2,24,512]{3,2,0,1:T(8,128)(2,1)S(1)}, bf16[32,2,24,512]{3,2,0,1:T(8,128)(2,1)}, u32[]{:S(2)}) copy-start(bf16[32,2,24,512]{3,2,0,1:T(8,128)(2,1)} %copy-done.6) | copy-start | bytes 4718596
  299.1 14.0 %slice-start = ((s8[6291456]{0:T(1024)(128)(4,1)}), s8[4194304]{0:T(1024)(128)(4,1)S(1)}, s32[]{:S(2)}) async-start(s8[6291456]{0:T(1024)(128)(4,1)} %bitcast.149), calls=%async_computation.3 | async-start | bytes 8388608
  308.0 5.1 slice-start.1
  313.1 122.4 %copy-start.2 = (bf16[1,128,2048]{2,1,0:T(8,128)(2,1)S(1)}, bf16[1,128,2048]{2,1,0:T(8,128)(2,1)}, u32[]{:S(2)}) copy-start(bf16[1,128,2048]{2,1,0:T(8,128)(2,1)} %param.8) | copy-start | bytes 1572868
  313.1 122.4 %copy-start.10 = (f32[8,1,256]{2,1,0:T(1,128)S(1)}, f32[8,1,256]{2,1,0:T(1,128)}, u32[]{:S(2)}) copy-start(f32[8,1,256]{2,1,0:T(1,128)} %copy-done.9) | copy-start | bytes 24580
  313.1 122.4 %copy-start.12 = (f32[128]{0:T(128)S(1)}, f32[128]{0:T(128)}, u32[]{:S(2)}) copy-start(f32[128]{0:T(128)} %copy-done.11) | copy-start | bytes 1540
  435.5 73.6 %copy-start.5 = (bf16[1,128,2048]{2,1,0:T(8,128)(2,1)S(1)}, bf16[1,128,2048]{2,1,0:T(8,128)(2,1)}, u32[]{:S(2)}) copy-start(bf16[1,128,2048]{2,1,0:T(8,128)(2,1)} %param.9) | copy-start | bytes 1572868
Sparse Core Ops, SparseCore 0:
  21.8 117.1 all-gather.10
  142.0 114.1 all-gather.8
